TPU v7x, 32 devices: a whole 2x2x4 slice. The times are simulated.
32 devices in a mesh: narrow: 4 (over y, core), wide: 8 (over z, x).
Axes of the slice: x: 2, y: 2, z: 4, core: 2. Of those that a mesh axis runs over, the one named last changes fastest.
Arguments:
- rhs_field: float32 [2, 32768, 768], P(None, ('wide', 'narrow')), may hold values from -6 to 6
- leaf_inverse: float32 [2, 32768, 512], P(None, ('wide', 'narrow')), may hold values from -0.1875 to 0.1875
- expand_one: float32 [2, 32768, 128], P(None, ('wide', 'narrow')), may hold values from -0.375 to 0.375
- project_one: float32 [2, 32768, 128], P(None, ('wide', 'narrow')), may hold values from -0.0625 to 0.0625
- core_one: float32 [2, 1024, 256], P(None, 'wide'), may hold values from -0.25 to 0.25
- expand_two: float32 [2, 32768, 128], P(None, ('wide', 'narrow')), may hold values from -0.375 to 0.375
- project_two: float32 [2, 32768, 128], P(None, ('wide', 'narrow')), may hold values from -0.046875 to 0.046875
- core_two: float32 [2, 512, 256], replicated, may hold values from -0.25 to 0.25
- expand_three: float32 [2, 32768, 128], P(None, ('wide', 'narrow')), may hold values from -0.375 to 0.375
- project_three: float32 [2, 32768, 128], P(None, ('wide', 'narrow')), may hold values from -0.03125 to 0.03125
- core_three: float32 [2, 256, 256], replicated, may hold values from -0.25 to 0.25
Outputs:
- solution: float32 [2, 32768, 768], P(None, ('wide', 'narrow'))
All inputs are finite; a program needn't handle non-finite values.
Results may differ from a plain program's by a relative error of at most 0.0003.
Values sent between devices are 32-bit elements; how exact they have to be, the bound alone decides.
No kernel may reach another device: no remote copies, remote signals or barrier semaphores. Data moves between devices by JAX's collectives and lax.ppermute only.
A program may use at most 128 MiB of HBM per device.

v0:
```python
import functools

import jax
import jax.numpy as jnp
from jax import lax
from jax.experimental import pallas as pl
from jax.experimental.pallas import tpu as pltpu
from jax.sharding import PartitionSpec as P


F32 = jnp.float32
BF16 = jnp.bfloat16
CHUNKS = 2


def swapped(array, axis, bit):
    return lax.ppermute(array, axis, [(i, i ^ 1 << bit) for i in range(lax.axis_size(axis))])


def split(value):
    high = value.astype(BF16)
    return high, (value - high.astype(F32)).astype(BF16)


def dot_nn(left, right):
    return lax.dot_general(left, right, (((1,), (0,)), ((), ())), preferred_element_type=F32)


def dot_nt(left, right):
    return lax.dot_general(left, right, (((1,), (1,)), ((), ())), preferred_element_type=F32)


def three_pass(dot, left, right):
    return dot(left[0], right[0]) + dot(left[0], right[1]) + dot(left[1], right[0])


def bits_of(size):
    return size.bit_length() - 1


def column_code():
    code = 0
    narrow = lax.axis_index("narrow")
    for bit in range(bits_of(lax.axis_size("narrow"))):
        code = code * 2 + (narrow >> bit) % 2
    return code * 2 + lax.axis_index("wide") % 2


def gram_kernel(pieces, p_two, p_three, e_one, e_two, kept, sent, held, full_two, full_three, arrived):
    rank = p_two.shape[2]
    half = rank // 2
    rows = p_two.shape[1] // pieces
    copies = [
        [
            pltpu.make_async_copy(
                array.at[:, piece * rows : (piece + 1) * rows],
                held.at[which, :, piece * rows : (piece + 1) * rows],
                arrived.at[piece, which],
            )
            for which, array in enumerate((e_one, e_two, p_two, p_three))
        ]
        for piece in range(pieces)
    ]
    for group in copies:
        for copy in group:
            copy.start()
    for piece, group in enumerate(copies):
        for copy in group:
            copy.wait()
        one, two, three, four = (
            [held[which, part, piece * rows : (piece + 1) * rows] for part in range(2)] for which in range(4)
        )
        right = split(jnp.concatenate([*one, *two], axis=1))
        near = tuple(part[:, : 2 * rank] for part in right)
        lower = three_pass(dot_nn, split(jnp.concatenate([three[0].T, three[1].T], axis=0)), near)
        upper = three_pass(dot_nn, split(jnp.concatenate([four[0].T, four[1].T], axis=0)), right)
        full_two[...] = lower if piece == 0 else full_two[...] + lower
        full_three[...] = upper if piece == 0 else full_three[...] + upper

    side = lax.axis_index("narrow") % 2
    place = 0
    for full, at in ((full_two, 0), (full_three, 0), (full_three, 2 * rank)):
        for flip in range(2):
            for target, which in ((kept, side), (sent, 1 - side)):
                upper = pl.ds(pl.multiple_of(which * half, half), half)
                lower = pl.ds(pl.multiple_of(rank + which * half, half), half)
                one = full[upper, at + flip * rank : at + (flip + 1) * rank]
                two = full[lower, at + (1 - flip) * rank : at + (2 - flip) * rank]
                target[:, place * rank : (place + 1) * rank] = one + two if flip == 0 else one - two
            place += 1


def leaf_kernel(blocks, chunk, inverse_far, source_far, one_far, two_far, three_far, *rest):
    solved, kept, sent, inverse, source, bases, x_high, x_low, total, source_in, inverse_in, bases_in = rest[-12:]
    step = pl.program_id(0)
    columns = source.shape[3]
    order = source.shape[2]
    leaves = source.shape[0]
    tiles = inverse_in.shape[0]
    tile = inverse.shape[1] // tiles
    per_leaf = tiles // leaves

    def source_copy(leaf):
        rows = pl.ds(pl.multiple_of(leaf * order, order), order)
        far = source_far.at[:, rows, chunk * columns : (chunk + 1) * columns]
        return pltpu.make_async_copy(far, source.at[leaf], source_in.at[leaf])

    def tile_copies(at):
        rows = pl.ds(pl.multiple_of(at * tile, tile), tile)
        yield pltpu.make_async_copy(inverse_far.at[:, rows], inverse.at[:, rows], inverse_in.at[at])
        for level, far in enumerate((one_far, two_far, three_far)):
            yield pltpu.make_async_copy(far.at[:, rows], bases.at[level, :, rows], bases_in.at[level, at])

    @pl.when(step == 0)
    def _():
        for at in range(tiles):
            if at % per_leaf == 0:
                source_copy(at // per_leaf).start()
            for copy in tile_copies(at):
                copy.start()

    @pl.when(step % per_leaf == 0)
    def _():
        leaf = step // per_leaf
        source_copy(leaf).wait()
        real, imag = source[leaf, 0], source[leaf, 1]
        for row, (first, second) in enumerate(((real, imag), (-imag, real))):
            high, low = split(jnp.concatenate([first, second], axis=1))
            x_high[row * order : (row + 1) * order] = high
            x_low[row * order : (row + 1) * order] = low

    for copy in tile_copies(step):
        copy.wait()
    here = pl.ds(pl.multiple_of(step * tile, tile), tile)

    @pl.when(step == 0)
    def _():
        total[...] = jnp.zeros_like(total)

    inverse_split = split(jnp.concatenate([inverse[0, here], inverse[1, here]], axis=1))
    y = three_pass(dot_nn, inverse_split, (x_high[...], x_low[...]))
    solved[0, here] = y[:, :columns]
    solved[1, here] = y[:, columns:]
    real_high, real_low = split(y[:, :columns].T)
    imag_high, imag_low = split(y[:, columns:].T)
    first, second = [], []
    for level in range(bases.shape[0]):
        real, imag = bases[level, 0, here], bases[level, 1, here]
        first += [real, -imag]
        second += [imag, real]
    first_high, first_low = split(jnp.concatenate(first, axis=1))
    second_high, second_low = split(jnp.concatenate(second, axis=1))
    left = jnp.concatenate([real_high, imag_high, real_high, imag_high, real_low, imag_low], axis=1)
    right = jnp.concatenate([first_high, second_high, first_low, second_low, first_high, second_high], axis=0)
    total[...] += dot_nn(left, right)

    @pl.when(step == pl.num_programs(0) - 1)
    def _():
        size = columns // blocks
        code = column_code()
        for place in range(blocks):
            rows = pl.ds(pl.multiple_of((code ^ place) * size, size), size)
            target, at = (kept, place) if place < blocks // 2 else (sent, place - blocks // 2)
            target[at * size : (at + 1) * size] = total[rows]


def complex_rows(real, imag):
    return jnp.concatenate(
        [jnp.concatenate([real, -imag], axis=1), jnp.concatenate([imag, real], axis=1)], axis=0
    )


def weights_kernel(mine, other, core_one, core_two, core_three, *outs):
    rank = core_one.shape[1]
    half = rank // 2
    scratch = outs[-1]
    side = lax.axis_index("narrow") % 2
    scratch[pl.ds(pl.multiple_of(side * half, half), half)] = mine[...]
    scratch[pl.ds(pl.multiple_of((1 - side) * half, half), half)] = other[...]
    wide = lax.axis_index("wide")
    wide_bits = bits_of(lax.axis_size("wide"))
    two = wide >> (wide_bits - 2)
    three = wide >> (wide_bits - 1)

    def piece(index):
        return scratch[:, index * rank : (index + 1) * rank]

    def store(index, value):
        high, low = split(value)
        outs[2 * index][...] = high
        outs[2 * index + 1][...] = low

    def lanes(ref, part, row, child):
        at = pl.ds(pl.multiple_of(child * rank, rank), rank)
        return ref[part, row, at]

    def own_rows(child):
        return pl.ds(pl.multiple_of(child * rank, rank), rank)

    everything = slice(None)
    odd = wide % 2
    left = odd == 0
    own = [[lanes(core_one, part, everything, (odd + k) % 2) for part in range(2)] for k in range(2)]
    sib_even = [piece(12), piece(14)]
    sib_odd = [piece(13), piece(15)]
    sib_own = [jnp.where(left, a, b) for a, b in zip(sib_even, sib_odd)]
    sib_sib = [jnp.where(left, b, a) for a, b in zip(sib_even, sib_odd)]
    store(
        0,
        jnp.concatenate(
            [
                jnp.concatenate([complex_rows(*own[0]), complex_rows(*own[1])], axis=1),
                jnp.concatenate([complex_rows(*sib_own), complex_rows(*sib_sib)], axis=1),
            ],
            axis=0,
        ),
    )
    store(
        1,
        jnp.concatenate(
            [
                jnp.concatenate([complex_rows(piece(0), piece(1)), complex_rows(piece(4), piece(5))], axis=1),
                jnp.concatenate([complex_rows(piece(2), piece(3)), complex_rows(piece(6), piece(7))], axis=1),
            ],
            axis=0,
        ),
    )

    def pair(ref, rows_child, side_of):
        rows = own_rows(rows_child)
        parts = [
            complex_rows(lanes(ref, 0, rows, (side_of + k) % 2), lanes(ref, 1, rows, (side_of + k) % 2)) for k in range(2)
        ]
        return jnp.concatenate(parts, axis=1)

    store(2, jnp.concatenate([pair(core_two, two, two % 2), pair(core_two, two ^ 1, two % 2)], axis=0))
    store(3, jnp.concatenate([complex_rows(piece(8), piece(9)), complex_rows(piece(10), piece(11))], axis=1))
    store(4, pair(core_three, three, three % 2))


def first_kernel(kept, got, w_high, w_low, g_high, g_low, coefficients, rest):
    width = kept.shape[1] // 3
    stacked = jnp.concatenate([kept[:, :width], got[:, :width]], axis=1)
    solved = three_pass(dot_nt, split(stacked), (w_high[...], w_low[...]))
    coefficients[...] = solved
    rest[...] = kept[:, width:] + got[:, width:] - three_pass(dot_nt, split(solved), (g_high[...], g_low[...]))


def second_kernel(mine, got, w_high, w_low, g_high, g_low, coefficients, rest):
    width = mine.shape[1] // 2
    stacked = jnp.concatenate([mine[:, :width], got[:, :width]], axis=1)
    solved = three_pass(dot_nt, split(stacked), (w_high[...], w_low[...]))
    coefficients[...] = solved[:, :width]
    rest[...] = mine[:, width:] + got[:, width:] - three_pass(dot_nt, split(solved), (g_high[...], g_low[...]))


def third_kernel(mine, got, w_high, w_low, one, two, kept, sent):
    width = mine.shape[1]
    stacked = jnp.concatenate([mine[...], got[...]], axis=1)
    three = three_pass(dot_nt, split(stacked), (w_high[...], w_low[...]))
    kept[:, :width] = one[:, :width]
    sent[:, :width] = one[:, width:]
    for target in (kept, sent):
        target[:, width : 2 * width] = two[...]
        target[:, 2 * width :] = three


def expand_kernel(blocks, solved, kept, got, e_one, e_two, e_three, *rest):
    out, natural, w_high, w_low = rest[-4:]
    columns = solved.shape[2]
    rank = e_one.shape[2]

    @pl.when(pl.program_id(0) == 0)
    def _():
        size = columns // blocks
        code = column_code()
        for place in range(blocks):
            rows = pl.ds(pl.multiple_of((code ^ place) * size, size), size)
            source, at = (kept, place) if place < blocks // 2 else (got, place - blocks // 2)
            natural[rows] = source[at * size : (at + 1) * size]
        for level in range(natural.shape[1] // (2 * rank)):
            here = slice(2 * level * rank, (2 * level + 1) * rank)
            there = slice((2 * level + 1) * rank, (2 * level + 2) * rank)
            real_high, real_low = split(natural[:, here])
            imag_high, imag_low = split(natural[:, there])
            for target, real, imag in ((w_high, real_high, imag_high), (w_low, real_low, imag_low)):
                target[:columns, here] = real
                target[:columns, there] = -imag
                target[columns:, here] = imag
                target[columns:, there] = real

    basis = []
    for e in (e_one, e_two, e_three):
        basis += [e[0], e[1]]
    update = three_pass(dot_nt, split(jnp.concatenate(basis, axis=1)), (w_high[...], w_low[...]))
    out[0] = solved[0] - update[:, :columns]
    out[1] = solved[1] - update[:, columns:]


def shape(*dims, dtype=F32):
    return jax.ShapeDtypeStruct(dims, dtype)


def estimate(flops, moved):
    return pl.CostEstimate(flops=int(flops), bytes_accessed=int(moved), transcendentals=0)


def params(mib):
    return pltpu.CompilerParams(vmem_limit_bytes=mib * 2**20)


def body(
    rhs_field,
    leaf_inverse,
    expand_one,
    project_one,
    core_one,
    expand_two,
    project_two,
    core_two,
    expand_three,
    project_three,
    core_three,
):
    def far_only(*arrays):
        return [pltpu.with_memory_space_constraint(array, pltpu.HBM) for array in arrays]

    rows, columns = rhs_field.shape[1:]
    order = leaf_inverse.shape[2]
    rank = project_one.shape[2]
    half = rank // 2
    narrow_bits = bits_of(lax.axis_size("narrow"))
    wide_bits = bits_of(lax.axis_size("wide"))
    blocks = 2 ** (narrow_bits + 1)
    part = columns // CHUNKS
    tile = order
    size = part // blocks
    lanes = 6 * rank

    far = pl.BlockSpec(memory_space=pltpu.HBM)

    def start(chunk, *after):
        return pl.pallas_call(
            functools.partial(leaf_kernel, blocks, chunk),
            grid=(rows // tile,),
            in_specs=[far] * 5 + [pl.BlockSpec(memory_space=pl.ANY)] * len(after),
            out_specs=[
                pl.BlockSpec((2, rows, part), lambda i: (0, 0, 0)),
                pl.BlockSpec((part // 2, lanes), lambda i: (0, 0)),
                pl.BlockSpec((part // 2, lanes), lambda i: (0, 0)),
            ],
            out_shape=[shape(2, rows, part), shape(part // 2, lanes), shape(part // 2, lanes)],
            scratch_shapes=[
                pltpu.VMEM((2, rows, order), F32),
                pltpu.VMEM((rows // order, 2, order, part), F32),
                pltpu.VMEM((3, 2, rows, rank), F32),
                pltpu.VMEM((2 * order, 2 * part), BF16),
                pltpu.VMEM((2 * order, 2 * part), BF16),
                pltpu.VMEM((part, lanes), F32),
                pltpu.SemaphoreType.DMA((rows // order,)),
                pltpu.SemaphoreType.DMA((rows // tile,)),
                pltpu.SemaphoreType.DMA((3, rows // tile)),
            ],
            compiler_params=params(40),
            cost_estimate=estimate(6 * rows * part * (4 * order + 12 * rank), 4 * rows * (2 * order + 2 * part)),
        )(*far_only(leaf_inverse, rhs_field, project_one, project_two, project_three), *after)

    def small(kernel, outs, after, *operands):
        def run(*refs):
            kernel(*refs[: len(operands)], *refs[len(operands) + len(after) :])

        return pl.pallas_call(
            run,
            in_specs=[pl.BlockSpec(memory_space=pltpu.VMEM)] * len(operands)
            + [pl.BlockSpec(memory_space=pl.ANY)] * len(after),
            out_shape=[shape(size, width * rank) for width in outs],
            compiler_params=params(16),
            cost_estimate=estimate(2 * 6 * size * 16 * rank * rank, 4 * 16 * rank * rank),
        )(*operands, *after)

    def columns_step(value, bit):
        middle = value.shape[0] // 2
        return value[:middle] + swapped(value[middle:], "narrow", bit)

    def first(value):
        kept, got = value[:size], swapped(value[size:], "wide", 0)
        return small(first_kernel, (4, 4), (), kept, got, *weights[:4])

    def second(rest, after):
        for bit in range(1, wide_bits - 2):
            rest = rest + swapped(rest, "wide", bit)
        got = swapped(rest, "wide", wide_bits - 2)
        return small(second_kernel, (2, 2), after, rest, got, *weights[4:8])

    def third(one, two, rest, after):
        got = swapped(rest, "wide", wide_bits - 1)
        return small(third_kernel, (6, 6), after, rest, got, *weights[8:], one, two)

    def grown(kept, got):
        return jnp.concatenate([kept, got], axis=0)

    def finish(chunk, solved, kept, got, before):
        step = order
        return pl.pallas_call(
            functools.partial(expand_kernel, blocks),
            grid=(rows // step,),
            in_specs=[
                pl.BlockSpec((2, step, part), lambda i: (0, i, 0)),
                pl.BlockSpec((part // 2, lanes), lambda i: (0, 0)),
                pl.BlockSpec((part // 2, lanes), lambda i: (0, 0)),
            ]
            + [pl.BlockSpec((2, step, rank), lambda i: (0, i, 0))] * 3
            + [pl.BlockSpec(memory_space=pl.ANY)] * len(before),
            out_specs=pl.BlockSpec((2, step, part), lambda i: (0, i, chunk)),
            out_shape=shape(2, rows, columns),
            input_output_aliases={6: 0} if before else {},
            scratch_shapes=[
                pltpu.VMEM((part, lanes), F32),
                pltpu.VMEM((2 * part, lanes), BF16),
                pltpu.VMEM((2 * part, lanes), BF16),
            ],
            compiler_params=params(32),
            cost_estimate=estimate(6 * rows * 2 * part * 6 * rank, 4 * rows * part * 4),
        )(solved, kept, got, expand_one, expand_two, expand_three, *before)

    half_gram = shape(half, lanes)
    pieces = 4
    gram, gram_sent = pl.pallas_call(
        functools.partial(gram_kernel, pieces),
        in_specs=[far] * 4,
        out_shape=[half_gram, half_gram],
        scratch_shapes=[
            pltpu.VMEM((4, 2, rows, rank), F32),
            pltpu.VMEM((2 * rank, 2 * rank), F32),
            pltpu.VMEM((2 * rank, 4 * rank), F32),
            pltpu.SemaphoreType.DMA((pieces, 4)),
        ],
        compiler_params=params(20),
        cost_estimate=estimate(2 * 3 * 12 * rank * rank * rows, 8 * rows * rank * 4),
        name="gram",
    )(*far_only(project_two, project_three, expand_one, expand_two))
    gram = gram + swapped(gram_sent, "narrow", 0)
    solved_a, kept, sent = start(0, gram)
    for bit in range(1, narrow_bits):
        gram = gram + swapped(gram, "narrow", bit)
    core_half = lax.dynamic_slice_in_dim(core_one, lax.axis_index("narrow") % 2 * half, half, 1)
    theirs = swapped(jnp.concatenate([gram, core_half[0], core_half[1]], axis=1), "wide", 0)
    a = kept + swapped(sent, "narrow", 0)
    solved_b, kept, sent = start(1, a, gram)
    for bit in range(1, narrow_bits):
        a = columns_step(a, bit)
    summed = gram[:, 4 * rank :] + theirs[:, 4 * rank : lanes]
    for bit in range(1, wide_bits - 2):
        summed = summed + swapped(summed, "wide", bit)
    summed_theirs = swapped(summed, "wide", wide_bits - 2)
    mine = jnp.concatenate(
        [gram[:, : 4 * rank], theirs[:, : 4 * rank], summed, summed_theirs, theirs[:, lanes:]], axis=1
    )
    other = swapped(mine, "narrow", 0)
    b = kept + swapped(sent, "narrow", 0)
    weight_dims = ((4, 4), (4, 4), (4, 4), (2, 4), (2, 4))
    weights = pl.pallas_call(
        weights_kernel,
        out_shape=[shape(a * rank, b * rank, dtype=BF16) for a, b in weight_dims for _ in range(2)],
        scratch_shapes=[pltpu.VMEM((rank, 16 * rank), F32)],
        compiler_params=params(24),
        cost_estimate=estimate(1e6, 6e6),
        name="weights",
    )(mine, other, core_one, core_two, core_three)

    one_a, a = first(a)
    for bit in range(1, narrow_bits):
        b = columns_step(b, bit)
    two_a, a = second(a, ())
    a, a_sent = third(one_a, two_a, a, ())
    one_b, b = first(b)
    a = grown(a, swapped(a_sent, "wide", 0))
    two_b, b = second(b, ())
    for bit in reversed(range(1, narrow_bits)):
        a = grown(a, swapped(a, "narrow", bit))
    b, b_sent = third(one_b, two_b, b, ())
    b = grown(b, swapped(b_sent, "wide", 0))
    out = finish(0, solved_a, a, swapped(a, "narrow", 0), [])
    for bit in reversed(range(1, narrow_bits)):
        b = grown(b, swapped(b, "narrow", bit))
    return finish(1, solved_b, b, swapped(b, "narrow", 0), [out])


def solution(mesh):
    placed = (
        P(None, ("wide", "narrow"), None),
        P(None, ("wide", "narrow"), None),
        P(None, ("wide", "narrow"), None),
        P(None, ("wide", "narrow"), None),
        P(None, "wide", None),
        P(None, ("wide", "narrow"), None),
        P(None, ("wide", "narrow"), None),
        P(),
        P(None, ("wide", "narrow"), None),
        P(None, ("wide", "narrow"), None),
        P(),
    )

    return jax.shard_map(
        body,
        mesh=mesh,
        in_specs=placed,
        out_specs=P(None, ("wide", "narrow"), None),
        check_vma=False,
    )
```

profile of v0, /device:TPU:0, one launch (start us, length us, event | category | flops | bytes accessed | tf_op | source)
XLA Modules:
  0.0 112.8 jit_solution(15039600502873032295)
XLA Ops:
  0.0 3.7 %gram.1 = (f32[64,768]{1,0:T(8,128)S(1)}, f32[64,768]{1,0:T(8,128)S(1)}) custom-call(f32[2,1024,128]{2,1,0:T(8,128)} %two_far.3, f32[2,1024,128]{2,1,0:T(8,128)} %three_far.3, f32[2,1024,128]{2,1,0:T(8,128)} %e_one.5, f32[2,1024,128]{2,1,0:T(8,128)} %e_two.5), custom_call_target="tpu_custom_call" | custom-call | flops 1207959552 | bytes 4194304 | tf_op jit(solution)/shard_map/gram/pallas_call | solution.py:428
  3.7 0.6 collective-permute-start
  4.3 1.1 collective-permute-done
  5.4 2.9 %collective-permute-start.2 = (f32[64,768]{1,0:T(8,128)S(1)}, f32[64,768]{1,0:T(8,128)S(1)}, u32[]{:S(2)}, u32[]{:S(2)}) collective-permute-start(f32[64,768]{1,0:T(8,128)S(1)} %add.28.rest_0_), channel_id=1, source_target_pairs={{0,16},{8,24},{16,0},{24,8},{1,17},{9,25},{17,1},{25,9},{2,18},{10... | collective-permute-start | bytes 589832 | tf_op jit(solution)/shard_map/ppermute | solution.py:17
  8.3 0.9 dynamic-slice_bitcast_fusion.1
  9.2 4.3 %collective-permute-done.2 = f32[64,768]{1,0:T(8,128)S(1)} collective-permute-done((f32[64,768]{1,0:T(8,128)S(1)}, f32[64,768]{1,0:T(8,128)S(1)}, u32[]{:S(2)}, u32[]{:S(2)}) %collective-permute-start.2) | collective-permute-done | bytes 196640 | tf_op jit(solution)/shard_map/ppermute | solution.py:17
  13.6 1.8 %collective-permute-start.6 = (f32[64,1280]{1,0:T(8,128)S(1)}, f32[64,1280]{1,0:T(8,128)S(1)}, u32[]{:S(2)}, u32[]{:S(2)}) collective-permute-start(f32[64,1280]{1,0:T(8,128)S(1)} %pad_maximum_fusion), channel_id=1, source_target_pairs={{0,1},{1,0},{2,3},{3,2},{4,5},{5,4},{6,7},{7,6},{8,9},{9,8},{10,11... | collective-permute-start | bytes 983048 | tf_op jit(solution)/shard_map/ppermute | solution.py:17
  15.4 14.2 %shard_map.109 = (f32[2,1024,384]{2,1,0:T(8,128)S(1)}, f32[192,768]{1,0:T(8,128)S(1)}, f32[192,768]{1,0:T(8,128)S(1)}) custom-call(f32[2,1024,512]{2,1,0:T(8,128)} %inverse_far.3, f32[2,1024,768]{2,1,0:T(8,128)} %source_far.3, f32[2,1024,128]{2,1,0:T(8,128)} %one_far.3, f32[2,1024,128]{2,1,0:T(8,128)} %two_far.3, f32[2,1024,128]{2,1,0:T(8,128)} %three_far.3, ...), custom_call_target="tpu_custom_call" | custom-call | flops 8455716864 | bytes 7340032 | tf_op jit(solution)/shard_map/pallas_call | solution.py:343
  29.5 0.1 collective-permute-start.1
  29.7 1.6 %collective-permute-start.7 = (f32[64,256]{1,0:T(8,128)S(1)}, f32[64,256]{1,0:T(8,128)S(1)}, u32[]{:S(2)}, u32[]{:S(2)}) collective-permute-start(f32[64,256]{1,0:T(8,128)S(1)} %get-tuple-element.66), channel_id=1, source_target_pairs={{0,2},{1,3},{2,0},{3,1},{4,6},{5,7},{6,4},{7,5},{8,10},{9,11},{10,... | collective-permute-start | bytes 196616 | tf_op jit(solution)/shard_map/ppermute | solution.py:17
  31.3 0.3 collective-permute-done.1
  31.6 0.1 add.29.rest_0_
  31.7 0.0 copy-start.5
  31.7 14.5 %shard_map.110 = (f32[2,1024,384]{2,1,0:T(8,128)S(1)}, f32[192,768]{1,0:T(8,128)S(1)}, f32[192,768]{1,0:T(8,128)S(1)}) custom-call(f32[2,1024,512]{2,1,0:T(8,128)} %inverse_far.3, f32[2,1024,768]{2,1,0:T(8,128)} %source_far.3, f32[2,1024,128]{2,1,0:T(8,128)} %one_far.3, f32[2,1024,128]{2,1,0:T(8,128)} %two_far.3, f32[2,1024,128]{2,1,0:T(8,128)} %three_far.3, ...), custom_call_target="tpu_custom_call" | custom-call | flops 8455716864 | bytes 7340032 | tf_op jit(solution)/shard_map/pallas_call | solution.py:343
  46.2 1.6 %collective-permute-start.14 = (f32[96,768]{1,0:T(8,128)S(1)}, f32[96,768]{1,0:T(8,128)S(1)}, u32[]{:S(2)}, u32[]{:S(2)}) collective-permute-start(f32[96,768]{1,0:T(8,128)S(1)} %slice.70), channel_id=1, source_target_pairs={{0,16},{8,24},{16,0},{24,8},{1,17},{9,25},{17,1},{25,9},{2,18},{10... | collective-permute-start | bytes 884744 | tf_op jit(solution)/shard_map/ppermute | solution.py:17
  47.8 0.6 collective-permute-start.8
  48.4 6.9 %collective-permute-done.14 = f32[96,768]{1,0:T(8,128)S(1)} collective-permute-done((f32[96,768]{1,0:T(8,128)S(1)}, f32[96,768]{1,0:T(8,128)S(1)}, u32[]{:S(2)}, u32[]{:S(2)}) %collective-permute-start.14) | collective-permute-done | bytes 294944 | tf_op jit(solution)/shard_map/ppermute | solution.py:17
  55.4 0.1 add.31
  55.5 1.6 %collective-permute-start.4 = (f32[96,768]{1,0:T(8,128)S(1)}, f32[96,768]{1,0:T(8,128)S(1)}, u32[]{:S(2)}, u32[]{:S(2)}) collective-permute-start(f32[96,768]{1,0:T(8,128)S(1)} %slice.61), channel_id=1, source_target_pairs={{0,16},{8,24},{16,0},{24,8},{1,17},{9,25},{17,1},{25,9},{2,18},{10... | collective-permute-start | bytes 884744 | tf_op jit(solution)/shard_map/ppermute | solution.py:17
  57.1 0.6 collective-permute-start.15
  57.7 1.0 weights.1
  58.7 3.6 %collective-permute-done.15.refs_1_ = f32[48,768]{1,0:T(8,128)S(1)} collective-permute-done((f32[48,768]{1,0:T(8,128)S(1)}, f32[48,768]{1,0:T(8,128)S(1)}, u32[]{:S(2)}, u32[]{:S(2)}) %collective-permute-start.15) | collective-permute-done | bytes 147488 | tf_op jit(solution)/shard_map/ppermute | solution.py:17
  62.3 1.1 shard_map.114
  63.4 1.6 %collective-permute-start.16 = (f32[48,512]{1,0:T(8,128)S(1)}, f32[48,512]{1,0:T(8,128)S(1)}, u32[]{:S(2)}, u32[]{:S(2)}) collective-permute-start(f32[48,512]{1,0:T(8,128)S(1)} %get-tuple-element.59.refs_0_), channel_id=1, source_target_pairs={{0,2},{1,3},{2,0},{3,1},{4,6},{5,7},{6,4},{7,5},{8,10},{9,11},{10,... | collective-permute-start | bytes 294920 | tf_op jit(solution)/shard_map/ppermute | solution.py:17
  65.1 0.6 collective-permute-start.5
  65.7 2.4 %collective-permute-done.16.refs_1_ = f32[48,512]{1,0:T(8,128)S(1)} collective-permute-done((f32[48,512]{1,0:T(8,128)S(1)}, f32[48,512]{1,0:T(8,128)S(1)}, u32[]{:S(2)}, u32[]{:S(2)}) %collective-permute-start.16) | collective-permute-done | bytes 98336 | tf_op jit(solution)/shard_map/ppermute | solution.py:17
  68.1 1.1 %shard_map.115 = (f32[48,256]{1,0:T(8,128)S(1)}, f32[48,256]{1,0:T(8,128)S(1)}) custom-call(f32[48,512]{1,0:T(8,128)S(1)} %get-tuple-element.59.refs_0_, f32[48,512]{1,0:T(8,128)S(1)} %collective-permute-done.16.refs_1_, bf16[512,512]{1,0:T(8,128)(2,1)S(1)} %get-tuple-element.47.refs_2_, bf16[512,512]{1,0:T(8,128)(2,1)S(1)} %get-tuple-element.48.refs_3_, ...), custom_call_target="tpu_custom_call" | custom-call | flops 150994944 | bytes 1048576 | tf_op jit(solution)/shard_map/pallas_call | solution.py:372
  69.2 2.7 %collective-permute-start.17 = (f32[48,256]{1,0:T(8,128)S(1)}, f32[48,256]{1,0:T(8,128)S(1)}, u32[]{:S(2)}, u32[]{:S(2)}) collective-permute-start(f32[48,256]{1,0:T(8,128)S(1)} %get-tuple-element.60.refs_0_), channel_id=1, source_target_pairs={{0,4},{1,5},{2,6},{3,7},{4,0},{5,1},{6,2},{7,3},{8,12},{9,13},{10,... | collective-permute-start | bytes 147464 | tf_op jit(solution)/shard_map/ppermute | solution.py:17
  71.9 2.4 %collective-permute-done.17.refs_1_ = f32[48,256]{1,0:T(8,128)S(1)} collective-permute-done((f32[48,256]{1,0:T(8,128)S(1)}, f32[48,256]{1,0:T(8,128)S(1)}, u32[]{:S(2)}, u32[]{:S(2)}) %collective-permute-start.17) | collective-permute-done | bytes 49184 | tf_op jit(solution)/shard_map/ppermute | solution.py:17
  74.3 0.3 shard_map.116
  74.6 0.6 collective-permute-start.18
  75.2 1.1 shard_map.111
  76.3 1.6 %collective-permute-start.9 = (f32[48,512]{1,0:T(8,128)S(1)}, f32[48,512]{1,0:T(8,128)S(1)}, u32[]{:S(2)}, u32[]{:S(2)}) collective-permute-start(f32[48,512]{1,0:T(8,128)S(1)} %get-tuple-element.46.refs_0_), channel_id=1, source_target_pairs={{0,2},{1,3},{2,0},{3,1},{4,6},{5,7},{6,4},{7,5},{8,10},{9,11},{10,... | collective-permute-start | bytes 294920 | tf_op jit(solution)/shard_map/ppermute | solution.py:17
  78.0 3.6 %collective-permute-done.9.refs_1_ = f32[48,512]{1,0:T(8,128)S(1)} collective-permute-done((f32[48,512]{1,0:T(8,128)S(1)}, f32[48,512]{1,0:T(8,128)S(1)}, u32[]{:S(2)}, u32[]{:S(2)}) %collective-permute-start.9) | collective-permute-done | bytes 98336 | tf_op jit(solution)/shard_map/ppermute | solution.py:17
  81.5 1.1 %shard_map.112 = (f32[48,256]{1,0:T(8,128)S(1)}, f32[48,256]{1,0:T(8,128)S(1)}) custom-call(f32[48,512]{1,0:T(8,128)S(1)} %get-tuple-element.46.refs_0_, f32[48,512]{1,0:T(8,128)S(1)} %collective-permute-done.9.refs_1_, bf16[512,512]{1,0:T(8,128)(2,1)S(1)} %get-tuple-element.47.refs_2_, bf16[512,512]{1,0:T(8,128)(2,1)S(1)} %get-tuple-element.48.refs_3_, ...), custom_call_target="tpu_custom_call" | custom-call | flops 150994944 | bytes 1048576 | tf_op jit(solution)/shard_map/pallas_call | solution.py:372
  82.7 2.2 %collective-permute-start.10 = (f32[48,256]{1,0:T(8,128)S(1)}, f32[48,256]{1,0:T(8,128)S(1)}, u32[]{:S(2)}, u32[]{:S(2)}) collective-permute-start(f32[48,256]{1,0:T(8,128)S(1)} %get-tuple-element.51.refs_0_), channel_id=1, source_target_pairs={{0,4},{1,5},{2,6},{3,7},{4,0},{5,1},{6,2},{7,3},{8,12},{9,13},{10,... | collective-permute-start | bytes 147464 | tf_op jit(solution)/shard_map/ppermute | solution.py:17
  84.9 0.6 collective-permute-start.19
  85.5 2.3 %collective-permute-done.10.refs_1_ = f32[48,256]{1,0:T(8,128)S(1)} collective-permute-done((f32[48,256]{1,0:T(8,128)S(1)}, f32[48,256]{1,0:T(8,128)S(1)}, u32[]{:S(2)}, u32[]{:S(2)}) %collective-permute-start.10) | collective-permute-done | bytes 49184 | tf_op jit(solution)/shard_map/ppermute | solution.py:17
  87.7 0.3 shard_map.113
  88.1 1.6 %collective-permute-start.11 = (f32[48,768]{1,0:T(8,128)S(1)}, f32[48,768]{1,0:T(8,128)S(1)}, u32[]{:S(2)}, u32[]{:S(2)}) collective-permute-start(f32[48,768]{1,0:T(8,128)S(1)} %get-tuple-element.57), channel_id=1, source_target_pairs={{0,1},{1,0},{2,3},{3,2},{4,5},{5,4},{6,7},{7,6},{8,9},{9,8},{10,11... | collective-permute-start | bytes 442376 | tf_op jit(solution)/shard_map/ppermute | solution.py:17
  89.7 3.6 %collective-permute-done.11 = f32[48,768]{1,0:T(8,128)S(1)} collective-permute-done((f32[48,768]{1,0:T(8,128)S(1)}, f32[48,768]{1,0:T(8,128)S(1)}, u32[]{:S(2)}, u32[]{:S(2)}) %collective-permute-start.11) | collective-permute-done | bytes 147488 | tf_op jit(solution)/shard_map/ppermute | solution.py:17
  93.3 0.4 collective-permute-start.12
  93.7 0.5 collective-permute-done.19
  94.2 0.1 collective-permute-start.20
  94.3 5.8 %collective-permute-done.12 = f32[96,768]{1,0:T(8,128)S(1)} collective-permute-done((f32[96,768]{1,0:T(8,128)S(1)}, f32[96,768]{1,0:T(8,128)S(1)}, u32[]{:S(2)}, u32[]{:S(2)}) %collective-permute-start.12) | collective-permute-done | bytes 294944 | tf_op jit(solution)/shard_map/ppermute | solution.py:17
  100.1 0.1 collective-permute-start.13
  100.2 6.3 %shard_map.117.rest_0_ = f32[2,1024,768]{2,1,0:T(8,128)} custom-call(f32[2,1024,384]{2,1,0:T(8,128)S(1)} %get-tuple-element.58.solved, f32[192,768]{1,0:T(8,128)S(1)} %constant_dynamic-update-slice_fusion.5.kept, f32[192,768]{1,0:T(8,128)S(1)} %collective-permute-done.20.got, f32[2,1024,128]{2,1,0:T(8,128)S(1)} %copy-done, f32[2,1024,128]{2,1,0:T(8,128)S(1)} %copy-done.1, ...), custom_call_target="tpu_custom_call" | custom-call | flops 3623878656 | bytes 6291456 | tf_op jit(solution)/shard_map/pallas_call | solution.py:404
  106.5 6.3 %shard_map.118 = f32[2,1024,768]{2,1,0:T(8,128)} custom-call(f32[2,1024,384]{2,1,0:T(8,128)S(1)} %get-tuple-element.39.solved, f32[192,768]{1,0:T(8,128)S(1)} %constant_dynamic-update-slice_fusion.2.kept, f32[192,768]{1,0:T(8,128)S(1)} %collective-permute-done.13.got, f32[2,1024,128]{2,1,0:T(8,128)S(1)} %copy-done, ...), custom_call_target="tpu_custom_call", output_to_operand_aliasing={{}: (6, {})} | custom-call | flops 3623878656 | bytes 6291456 | tf_op jit(solution)/shard_map/pallas_call | solution.py:404
  (43 shorter events, 0.5 us)
Async XLA Ops:
  3.7 1.6 %collective-permute-start = (f32[64,768]{1,0:T(8,128)S(1)}, f32[64,768]{1,0:T(8,128)S(1)}, u32[]{:S(2)}, u32[]{:S(2)}) collective-permute-start(f32[64,768]{1,0:T(8,128)S(1)} %get-tuple-element.36), channel_id=1, source_target_pairs={{0,8},{8,0},{16,24},{24,16},{1,9},{9,1},{17,25},{25,17},{2,10},{10... | collective-permute-start | bytes 589832 | tf_op jit(solution)/shard_map/ppermute | solution.py:17
  5.4 8.1 %collective-permute-start.2 = (f32[64,768]{1,0:T(8,128)S(1)}, f32[64,768]{1,0:T(8,128)S(1)}, u32[]{:S(2)}, u32[]{:S(2)}) collective-permute-start(f32[64,768]{1,0:T(8,128)S(1)} %add.28.rest_0_), channel_id=1, source_target_pairs={{0,16},{8,24},{16,0},{24,8},{1,17},{9,25},{17,1},{25,9},{2,18},{10... | collective-permute-start | bytes 589832 | tf_op jit(solution)/shard_map/ppermute | solution.py:17
  13.6 16.0 %collective-permute-start.6 = (f32[64,1280]{1,0:T(8,128)S(1)}, f32[64,1280]{1,0:T(8,128)S(1)}, u32[]{:S(2)}, u32[]{:S(2)}) collective-permute-start(f32[64,1280]{1,0:T(8,128)S(1)} %pad_maximum_fusion), channel_id=1, source_target_pairs={{0,1},{1,0},{2,3},{3,2},{4,5},{5,4},{6,7},{7,6},{8,9},{9,8},{10,11... | collective-permute-start | bytes 983048 | tf_op jit(solution)/shard_map/ppermute | solution.py:17
  29.5 2.1 %collective-permute-start.1 = (f32[192,768]{1,0:T(8,128)S(1)}, f32[192,768]{1,0:T(8,128)S(1)}, u32[]{:S(2)}, u32[]{:S(2)}) collective-permute-start(f32[192,768]{1,0:T(8,128)S(1)} %get-tuple-element.38), channel_id=1, source_target_pairs={{0,8},{8,0},{16,24},{24,16},{1,9},{9,1},{17,25},{25,17},{2,10},{10... | collective-permute-start | bytes 1769480 | tf_op jit(solution)/shard_map/ppermute | solution.py:17
  29.7 18.1 %collective-permute-start.7 = (f32[64,256]{1,0:T(8,128)S(1)}, f32[64,256]{1,0:T(8,128)S(1)}, u32[]{:S(2)}, u32[]{:S(2)}) collective-permute-start(f32[64,256]{1,0:T(8,128)S(1)} %get-tuple-element.66), channel_id=1, source_target_pairs={{0,2},{1,3},{2,0},{3,1},{4,6},{5,7},{6,4},{7,5},{8,10},{9,11},{10,... | collective-permute-start | bytes 196616 | tf_op jit(solution)/shard_map/ppermute | solution.py:17
  31.7 26.0 %copy-start.3 = (f32[2,512,256]{2,1,0:T(8,128)S(1)}, f32[2,512,256]{2,1,0:T(8,128)}, u32[]{:S(2)}) copy-start(f32[2,512,256]{2,1,0:T(8,128)} %core_two.1) | copy-start | bytes 3145732
  31.7 26.0 %copy-start.4 = (f32[2,128,256]{2,1,0:T(8,128)S(1)}, f32[2,128,256]{2,1,0:T(8,128)}, u32[]{:S(2)}) copy-start(f32[2,128,256]{2,1,0:T(8,128)} %core_one.1) | copy-start | bytes 786436
  31.7 26.0 %copy-start.5 = (f32[2,256,256]{2,1,0:T(8,128)S(1)}, f32[2,256,256]{2,1,0:T(8,128)}, u32[]{:S(2)}) copy-start(f32[2,256,256]{2,1,0:T(8,128)} %core_three.1) | copy-start | bytes 1572868
  46.2 9.1 %collective-permute-start.14 = (f32[96,768]{1,0:T(8,128)S(1)}, f32[96,768]{1,0:T(8,128)S(1)}, u32[]{:S(2)}, u32[]{:S(2)}) collective-permute-start(f32[96,768]{1,0:T(8,128)S(1)} %slice.70), channel_id=1, source_target_pairs={{0,16},{8,24},{16,0},{24,8},{1,17},{9,25},{17,1},{25,9},{2,18},{10... | collective-permute-start | bytes 884744 | tf_op jit(solution)/shard_map/ppermute | solution.py:17
  47.8 7.6 %collective-permute-start.3 = (f32[192,768]{1,0:T(8,128)S(1)}, f32[192,768]{1,0:T(8,128)S(1)}, u32[]{:S(2)}, u32[]{:S(2)}) collective-permute-start(f32[192,768]{1,0:T(8,128)S(1)} %get-tuple-element.41), channel_id=1, source_target_pairs={{0,8},{8,0},{16,24},{24,16},{1,9},{9,1},{17,25},{25,17},{2,10},{10... | collective-permute-start | bytes 1769480 | tf_op jit(solution)/shard_map/ppermute | solution.py:17
  47.8 9.9 %collective-permute-start.8 = (f32[64,2048]{1,0:T(8,128)S(1)}, f32[64,2048]{1,0:T(8,128)S(1)}, u32[]{:S(2)}, u32[]{:S(2)}) collective-permute-start(f32[64,2048]{1,0:T(8,128)S(1)} %slice_dynamic-update-slice_fusion.mine), channel_id=1, source_target_pairs={{0,8},{8,0},{16,24},{24,16},{1,9},{9,1},{17,25},{25,17},{2,10},{10... | collective-permute-start | bytes 1572872 | tf_op jit(solution)/shard_map/ppermute | solution.py:17
  55.5 9.6 %collective-permute-start.4 = (f32[96,768]{1,0:T(8,128)S(1)}, f32[96,768]{1,0:T(8,128)S(1)}, u32[]{:S(2)}, u32[]{:S(2)}) collective-permute-start(f32[96,768]{1,0:T(8,128)S(1)} %slice.61), channel_id=1, source_target_pairs={{0,16},{8,24},{16,0},{24,8},{1,17},{9,25},{17,1},{25,9},{2,18},{10... | collective-permute-start | bytes 884744 | tf_op jit(solution)/shard_map/ppermute | solution.py:17
  57.1 5.2 %collective-permute-start.15 = (f32[48,768]{1,0:T(8,128)S(1)}, f32[48,768]{1,0:T(8,128)S(1)}, u32[]{:S(2)}, u32[]{:S(2)}) collective-permute-start(f32[48,768]{1,0:T(8,128)S(1)} %get-tuple-element.67), channel_id=1, source_target_pairs={{0,1},{1,0},{2,3},{3,2},{4,5},{5,4},{6,7},{7,6},{8,9},{9,8},{10,11... | collective-permute-start | bytes 442376 | tf_op jit(solution)/shard_map/ppermute | solution.py:17
  63.4 36.8 %copy-start = (f32[2,1024,128]{2,1,0:T(8,128)S(1)}, f32[2,1024,128]{2,1,0:T(8,128)}, u32[]{:S(2)}) copy-start(f32[2,1024,128]{2,1,0:T(8,128)} %e_one.5) | copy-start | bytes 3145732
  63.4 36.8 %copy-start.1 = (f32[2,1024,128]{2,1,0:T(8,128)S(1)}, f32[2,1024,128]{2,1,0:T(8,128)}, u32[]{:S(2)}) copy-start(f32[2,1024,128]{2,1,0:T(8,128)} %e_two.5) | copy-start | bytes 3145732
  63.4 36.8 %copy-start.2 = (f32[2,1024,128]{2,1,0:T(8,128)S(1)}, f32[2,1024,128]{2,1,0:T(8,128)}, u32[]{:S(2)}) copy-start(f32[2,1024,128]{2,1,0:T(8,128)} %e_three.3) | copy-start | bytes 3145732
  63.4 4.7 %collective-permute-start.16 = (f32[48,512]{1,0:T(8,128)S(1)}, f32[48,512]{1,0:T(8,128)S(1)}, u32[]{:S(2)}, u32[]{:S(2)}) collective-permute-start(f32[48,512]{1,0:T(8,128)S(1)} %get-tuple-element.59.refs_0_), channel_id=1, source_target_pairs={{0,2},{1,3},{2,0},{3,1},{4,6},{5,7},{6,4},{7,5},{8,10},{9,11},{10,... | collective-permute-start | bytes 294920 | tf_op jit(solution)/shard_map/ppermute | solution.py:17
  65.1 10.1 %collective-permute-start.5 = (f32[48,768]{1,0:T(8,128)S(1)}, f32[48,768]{1,0:T(8,128)S(1)}, u32[]{:S(2)}, u32[]{:S(2)}) collective-permute-start(f32[48,768]{1,0:T(8,128)S(1)} %get-tuple-element.69), channel_id=1, source_target_pairs={{0,1},{1,0},{2,3},{3,2},{4,5},{5,4},{6,7},{7,6},{8,9},{9,8},{10,11... | collective-permute-start | bytes 442376 | tf_op jit(solution)/shard_map/ppermute | solution.py:17
  69.2 5.1 %collective-permute-start.17 = (f32[48,256]{1,0:T(8,128)S(1)}, f32[48,256]{1,0:T(8,128)S(1)}, u32[]{:S(2)}, u32[]{:S(2)}) collective-permute-start(f32[48,256]{1,0:T(8,128)S(1)} %get-tuple-element.60.refs_0_), channel_id=1, source_target_pairs={{0,4},{1,5},{2,6},{3,7},{4,0},{5,1},{6,2},{7,3},{8,12},{9,13},{10,... | collective-permute-start | bytes 147464 | tf_op jit(solution)/shard_map/ppermute | solution.py:17
  74.6 10.2 %collective-permute-start.18 = (f32[48,768]{1,0:T(8,128)S(1)}, f32[48,768]{1,0:T(8,128)S(1)}, u32[]{:S(2)}, u32[]{:S(2)}) collective-permute-start(f32[48,768]{1,0:T(8,128)S(1)} %get-tuple-element.64), channel_id=1, source_target_pairs={{0,1},{1,0},{2,3},{3,2},{4,5},{5,4},{6,7},{7,6},{8,9},{9,8},{10,11... | collective-permute-start | bytes 442376 | tf_op jit(solution)/shard_map/ppermute | solution.py:17
  76.3 5.2 %collective-permute-start.9 = (f32[48,512]{1,0:T(8,128)S(1)}, f32[48,512]{1,0:T(8,128)S(1)}, u32[]{:S(2)}, u32[]{:S(2)}) collective-permute-start(f32[48,512]{1,0:T(8,128)S(1)} %get-tuple-element.46.refs_0_), channel_id=1, source_target_pairs={{0,2},{1,3},{2,0},{3,1},{4,6},{5,7},{6,4},{7,5},{8,10},{9,11},{10,... | collective-permute-start | bytes 294920 | tf_op jit(solution)/shard_map/ppermute | solution.py:17
  82.7 5.1 %collective-permute-start.10 = (f32[48,256]{1,0:T(8,128)S(1)}, f32[48,256]{1,0:T(8,128)S(1)}, u32[]{:S(2)}, u32[]{:S(2)}) collective-permute-start(f32[48,256]{1,0:T(8,128)S(1)} %get-tuple-element.51.refs_0_), channel_id=1, source_target_pairs={{0,4},{1,5},{2,6},{3,7},{4,0},{5,1},{6,2},{7,3},{8,12},{9,13},{10,... | collective-permute-start | bytes 147464 | tf_op jit(solution)/shard_map/ppermute | solution.py:17
  84.9 9.3 %collective-permute-start.19 = (f32[96,768]{1,0:T(8,128)S(1)}, f32[96,768]{1,0:T(8,128)S(1)}, u32[]{:S(2)}, u32[]{:S(2)}) collective-permute-start(f32[96,768]{1,0:T(8,128)S(1)} %pad_maximum_fusion.2), channel_id=1, source_target_pairs={{0,16},{8,24},{16,0},{24,8},{1,17},{9,25},{17,1},{25,9},{2,18},{10... | collective-permute-start | bytes 884744 | tf_op jit(solution)/shard_map/ppermute | solution.py:17
  88.1 5.2 %collective-permute-start.11 = (f32[48,768]{1,0:T(8,128)S(1)}, f32[48,768]{1,0:T(8,128)S(1)}, u32[]{:S(2)}, u32[]{:S(2)}) collective-permute-start(f32[48,768]{1,0:T(8,128)S(1)} %get-tuple-element.57), channel_id=1, source_target_pairs={{0,1},{1,0},{2,3},{3,2},{4,5},{5,4},{6,7},{7,6},{8,9},{9,8},{10,11... | collective-permute-start | bytes 442376 | tf_op jit(solution)/shard_map/ppermute | solution.py:17
  93.3 6.8 %collective-permute-start.12 = (f32[96,768]{1,0:T(8,128)S(1)}, f32[96,768]{1,0:T(8,128)S(1)}, u32[]{:S(2)}, u32[]{:S(2)}) collective-permute-start(f32[96,768]{1,0:T(8,128)S(1)} %pad_maximum_fusion.1), channel_id=1, source_target_pairs={{0,16},{8,24},{16,0},{24,8},{1,17},{9,25},{17,1},{25,9},{2,18},{10... | collective-permute-start | bytes 884744 | tf_op jit(solution)/shard_map/ppermute | solution.py:17
  94.2 6.0 %collective-permute-start.20 = (f32[192,768]{1,0:T(8,128)S(1)}, f32[192,768]{1,0:T(8,128)S(1)}, u32[]{:S(2)}, u32[]{:S(2)}) collective-permute-start(f32[192,768]{1,0:T(8,128)S(1)} %constant_dynamic-update-slice_fusion.5.kept), channel_id=1, source_target_pairs={{0,8},{8,0},{16,24},{24,16},{1,9},{9,1},{17,25},{25,17},{2,10},{10... | collective-permute-start | bytes 1769480 | tf_op jit(solution)/shard_map/ppermute | solution.py:17
  100.1 6.4 %collective-permute-start.13 = (f32[192,768]{1,0:T(8,128)S(1)}, f32[192,768]{1,0:T(8,128)S(1)}, u32[]{:S(2)}, u32[]{:S(2)}) collective-permute-start(f32[192,768]{1,0:T(8,128)S(1)} %constant_dynamic-update-slice_fusion.2.kept), channel_id=1, source_target_pairs={{0,8},{8,0},{16,24},{24,16},{1,9},{9,1},{17,25},{25,17},{2,10},{10... | collective-permute-start | bytes 1769480 | tf_op jit(solution)/shard_map/ppermute | solution.py:17
where the time goes:
time: 113 us
  Pallas kernels  51 us (45%)
  waiting for transfers between devices  36.7 us (32%)
  starting transfers between devices  23.3 us (21%)
    ppermute x21, waiting for transfers between devices, swapped(): lax.ppermute(array, axis, [(i, i ^ 1 << bit) for i in range(lax.axis_size...  36.7 us
    pallas_call x2, Pallas kernels, start(): pl.pallas_call(functools.partial(leaf_kernel, blocks, chunk), grid=(rows...  28.6 us
    ppermute x21, starting transfers between devices, swapped(): lax.ppermute(array, axis, [(i, i ^ 1 << bit) for i in range(lax.axis_size...  23.3 us
    pallas_call x2, Pallas kernels, finish(): pl.pallas_call(functools.partial(expand_kernel, blocks), grid=(rows // st...  12.5 us
    pallas_call x6, Pallas kernels, small(): pl.pallas_call(run, in_specs=[pl.BlockSpec(memory_space=pltpu.VMEM)] * le...  5.08 us
    pallas_call x1, Pallas kernels, body(): pl.pallas_call(functools.partial(gram_kernel, pieces), in_specs=[far] * 4...  3.73 us
  transfers between devices with their start and end apart: 21, of which 12 were waited for; matrix products, arithmetic and copies ran while one was open for 1% of the time, Pallas kernels for 36%

commit v1 on v0

--- a/solution.py
+++ b/solution.py
@@ -170,72 +170,61 @@
     )
 
 
-def weights_kernel(mine, other, core_one, core_two, core_three, *outs):
+def joined(mine, other, whole):
+    half = mine.shape[0]
+    side = lax.axis_index("narrow") % 2
+    whole[pl.ds(pl.multiple_of(side * half, half), half)] = mine[...]
+    whole[pl.ds(pl.multiple_of((1 - side) * half, half), half)] = other[...]
+
+
+def store(high_ref, low_ref, value):
+    high_ref[...], low_ref[...] = split(value)
+
+
+def lane_block(ref, part, rows, child, rank):
+    return ref[part, rows, pl.ds(pl.multiple_of(child * rank, rank), rank)]
+
+
+def near_weights_kernel(mine, other, core_one, core_high, core_low, gram_high, gram_low, whole):
     rank = core_one.shape[1]
-    half = rank // 2
-    scratch = outs[-1]
-    side = lax.axis_index("narrow") % 2
-    scratch[pl.ds(pl.multiple_of(side * half, half), half)] = mine[...]
-    scratch[pl.ds(pl.multiple_of((1 - side) * half, half), half)] = other[...]
+    joined(mine, other, whole)
+    odd = lax.axis_index("wide") % 2
+
+    def piece(index):
+        return whole[:, index * rank : (index + 1) * rank]
+
+    own = [[lane_block(core_one, part, slice(None), (odd + k) % 2, rank) for part in range(2)] for k in range(2)]
+    even_first = odd == 0
+    sib_own = [jnp.where(even_first, piece(8 + 2 * part), piece(9 + 2 * part)) for part in range(2)]
+    sib_sib = [jnp.where(even_first, piece(9 + 2 * part), piece(8 + 2 * part)) for part in range(2)]
+    upper = jnp.concatenate([complex_rows(*own[0]), complex_rows(*own[1])], axis=1)
+    lower = jnp.concatenate([complex_rows(*sib_own), complex_rows(*sib_sib)], axis=1)
+    store(core_high, core_low, jnp.concatenate([upper, lower], axis=0))
+    upper = jnp.concatenate([complex_rows(piece(0), piece(1)), complex_rows(piece(4), piece(5))], axis=1)
+    lower = jnp.concatenate([complex_rows(piece(2), piece(3)), complex_rows(piece(6), piece(7))], axis=1)
+    store(gram_high, gram_low, jnp.concatenate([upper, lower], axis=0))
+
+
+def far_weights_kernel(mine, other, core_two, core_three, *outs):
+    whole = outs[-1]
+    rank = whole.shape[0]
+    joined(mine, other, whole)
     wide = lax.axis_index("wide")
     wide_bits = bits_of(lax.axis_size("wide"))
     two = wide >> (wide_bits - 2)
     three = wide >> (wide_bits - 1)
 
     def piece(index):
-        return scratch[:, index * rank : (index + 1) * rank]
-
-    def store(index, value):
-        high, low = split(value)
-        outs[2 * index][...] = high
-        outs[2 * index + 1][...] = low
-
-    def lanes(ref, part, row, child):
-        at = pl.ds(pl.multiple_of(child * rank, rank), rank)
-        return ref[part, row, at]
-
-    def own_rows(child):
-        return pl.ds(pl.multiple_of(child * rank, rank), rank)
-
-    everything = slice(None)
-    odd = wide % 2
-    left = odd == 0
-    own = [[lanes(core_one, part, everything, (odd + k) % 2) for part in range(2)] for k in range(2)]
-    sib_even = [piece(12), piece(14)]
-    sib_odd = [piece(13), piece(15)]
-    sib_own = [jnp.where(left, a, b) for a, b in zip(sib_even, sib_odd)]
-    sib_sib = [jnp.where(left, b, a) for a, b in zip(sib_even, sib_odd)]
-    store(
-        0,
-        jnp.concatenate(
-            [
-                jnp.concatenate([complex_rows(*own[0]), complex_rows(*own[1])], axis=1),
-                jnp.concatenate([complex_rows(*sib_own), complex_rows(*sib_sib)], axis=1),
-            ],
-            axis=0,
-        ),
-    )
-    store(
-        1,
-        jnp.concatenate(
-            [
-                jnp.concatenate([complex_rows(piece(0), piece(1)), complex_rows(piece(4), piece(5))], axis=1),
-                jnp.concatenate([complex_rows(piece(2), piece(3)), complex_rows(piece(6), piece(7))], axis=1),
-            ],
-            axis=0,
-        ),
-    )
-
-    def pair(ref, rows_child, side_of):
-        rows = own_rows(rows_child)
-        parts = [
-            complex_rows(lanes(ref, 0, rows, (side_of + k) % 2), lanes(ref, 1, rows, (side_of + k) % 2)) for k in range(2)
-        ]
-        return jnp.concatenate(parts, axis=1)
-
-    store(2, jnp.concatenate([pair(core_two, two, two % 2), pair(core_two, two ^ 1, two % 2)], axis=0))
-    store(3, jnp.concatenate([complex_rows(piece(8), piece(9)), complex_rows(piece(10), piece(11))], axis=1))
-    store(4, pair(core_three, three, three % 2))
+        return whole[:, index * rank : (index + 1) * rank]
+
+    def pair(ref, child, side):
+        rows = pl.ds(pl.multiple_of(child * rank, rank), rank)
+        parts = [[lane_block(ref, part, rows, (side + k) % 2, rank) for part in range(2)] for k in range(2)]
+        return jnp.concatenate([complex_rows(*parts[0]), complex_rows(*parts[1])], axis=1)
+
+    store(outs[0], outs[1], jnp.concatenate([pair(core_two, two, two % 2), pair(core_two, two ^ 1, two % 2)], axis=0))
+    store(outs[2], outs[3], jnp.concatenate([complex_rows(piece(0), piece(1)), complex_rows(piece(2), piece(3))], axis=1))
+    store(outs[4], outs[5], pair(core_three, three, three % 2))
 
 
 def first_kernel(kept, got, w_high, w_low, g_high, g_low, coefficients, rest):
@@ -449,24 +438,26 @@
     solved_b, kept, sent = start(1, a, gram)
     for bit in range(1, narrow_bits):
         a = columns_step(a, bit)
+    b = kept + swapped(sent, "narrow", 0)
+
+    def weights_of(kernel, dims, blocks_held, *operands):
+        return pl.pallas_call(
+            kernel,
+            out_shape=[shape(i * rank, j * rank, dtype=BF16) for i, j in dims for _ in range(2)],
+            scratch_shapes=[pltpu.VMEM((rank, blocks_held * rank), F32)],
+            compiler_params=params(24),
+            cost_estimate=estimate(1e6, 3e6),
+        )(*operands)
+
+    mine = jnp.concatenate([gram[:, : 4 * rank], theirs[:, : 4 * rank], theirs[:, lanes:]], axis=1)
+    near = weights_of(near_weights_kernel, ((4, 4), (4, 4)), 12, mine, swapped(mine, "narrow", 0), core_one)
     summed = gram[:, 4 * rank :] + theirs[:, 4 * rank : lanes]
     for bit in range(1, wide_bits - 2):
         summed = summed + swapped(summed, "wide", bit)
-    summed_theirs = swapped(summed, "wide", wide_bits - 2)
-    mine = jnp.concatenate(
-        [gram[:, : 4 * rank], theirs[:, : 4 * rank], summed, summed_theirs, theirs[:, lanes:]], axis=1
-    )
+    mine = jnp.concatenate([summed, swapped(summed, "wide", wide_bits - 2)], axis=1)
     other = swapped(mine, "narrow", 0)
-    b = kept + swapped(sent, "narrow", 0)
-    weight_dims = ((4, 4), (4, 4), (4, 4), (2, 4), (2, 4))
-    weights = pl.pallas_call(
-        weights_kernel,
-        out_shape=[shape(a * rank, b * rank, dtype=BF16) for a, b in weight_dims for _ in range(2)],
-        scratch_shapes=[pltpu.VMEM((rank, 16 * rank), F32)],
-        compiler_params=params(24),
-        cost_estimate=estimate(1e6, 6e6),
-        name="weights",
-    )(mine, other, core_one, core_two, core_three)
+    coarse = weights_of(far_weights_kernel, ((4, 4), (2, 4), (2, 4)), 4, mine, other, core_two, core_three)
+    weights = [*near, *coarse]
 
     one_a, a = first(a)
     for bit in range(1, narrow_bits):

time: 113 us -> 115 us (1.018)
  waiting for transfers between devices: 36.7 us -> 39.2 us
    ppermute x21 -> x22, waiting for transfers between devices: 36.7 us -> 39.2 us  [swapped(): lax.ppermute(array, axis, [(i, i ^ 1 << bit) for i in range(lax.axis_size...]
    ppermute x21 -> x22, starting transfers between devices: 23.3 us -> 23.2 us  [swapped(): lax.ppermute(array, axis, [(i, i ^ 1 << bit) for i in range(lax.axis_size...]
  transfers between devices with their start and end apart: 21 -> 22, of which waited for: 12 -> 11; matrix products, arithmetic and copies ran while one was open for 1% -> 1% of each run, Pallas kernels for 36% -> 36%
where the time goes in v1:
time: 115 us
  Pallas kernels  50.9 us (44%)
  waiting for transfers between devices  39.2 us (34%)
  starting transfers between devices  23.2 us (20%)
    ppermute x22, waiting for transfers between devices, swapped(): lax.ppermute(array, axis, [(i, i ^ 1 << bit) for i in range(lax.axis_size...  39.2 us
    pallas_call x2, Pallas kernels, start(): pl.pallas_call(functools.partial(leaf_kernel, blocks, chunk), grid=(rows...  28.5 us
    ppermute x22, starting transfers between devices, swapped(): lax.ppermute(array, axis, [(i, i ^ 1 << bit) for i in range(lax.axis_size...  23.2 us
    pallas_call x2, Pallas kernels, finish(): pl.pallas_call(functools.partial(expand_kernel, blocks), grid=(rows // st...  12.5 us
    pallas_call x6, Pallas kernels, small(): pl.pallas_call(run, in_specs=[pl.BlockSpec(memory_space=pltpu.VMEM)] * le...  5.08 us
    pallas_call x1, Pallas kernels, body(): pl.pallas_call(functools.partial(gram_kernel, pieces), in_specs=[far] * 4...  3.73 us
  transfers between devices with their start and end apart: 22, of which 11 were waited for; matrix products, arithmetic and copies ran while one was open for 1% of the time, Pallas kernels for 36%

profile of v1, /device:TPU:0, one launch (start us, length us, event | category | flops | bytes accessed | tf_op | source)
XLA Modules:
  0.0 115.1 jit_solution(18263386747283086943)
XLA Ops:
  0.0 3.7 %gram.1 = (f32[64,768]{1,0:T(8,128)S(1)}, f32[64,768]{1,0:T(8,128)S(1)}) custom-call(f32[2,1024,128]{2,1,0:T(8,128)} %two_far.3, f32[2,1024,128]{2,1,0:T(8,128)} %three_far.3, f32[2,1024,128]{2,1,0:T(8,128)} %e_one.5, f32[2,1024,128]{2,1,0:T(8,128)} %e_two.5), custom_call_target="tpu_custom_call" | custom-call | flops 1207959552 | bytes 4194304 | tf_op jit(solution)/shard_map/gram/pallas_call | solution.py:417
  3.7 0.6 collective-permute-start
  4.3 0.9 dynamic-slice_bitcast_fusion.1
  5.2 0.2 collective-permute-done
  5.4 2.9 %collective-permute-start.2 = (f32[64,768]{1,0:T(8,128)S(1)}, f32[64,768]{1,0:T(8,128)S(1)}, u32[]{:S(2)}, u32[]{:S(2)}) collective-permute-start(f32[64,768]{1,0:T(8,128)S(1)} %add.28.rest_0_), channel_id=1, source_target_pairs={{0,16},{8,24},{16,0},{24,8},{1,17},{9,25},{17,1},{25,9},{2,18},{10... | collective-permute-start | bytes 589832 | tf_op jit(solution)/shard_map/ppermute | solution.py:17
  8.3 14.2 %shard_map.109 = (f32[2,1024,384]{2,1,0:T(8,128)S(1)}, f32[192,768]{1,0:T(8,128)S(1)}, f32[192,768]{1,0:T(8,128)S(1)}) custom-call(f32[2,1024,512]{2,1,0:T(8,128)} %inverse_far.3, f32[2,1024,768]{2,1,0:T(8,128)} %source_far.3, f32[2,1024,128]{2,1,0:T(8,128)} %one_far.3, f32[2,1024,128]{2,1,0:T(8,128)} %two_far.3, f32[2,1024,128]{2,1,0:T(8,128)} %three_far.3, ...), custom_call_target="tpu_custom_call" | custom-call | flops 8455716864 | bytes 7340032 | tf_op jit(solution)/shard_map/pallas_call | solution.py:332
  22.5 0.1 collective-permute-start.1
  22.6 1.6 %collective-permute-start.6 = (f32[64,1280]{1,0:T(8,128)S(1)}, f32[64,1280]{1,0:T(8,128)S(1)}, u32[]{:S(2)}, u32[]{:S(2)}) collective-permute-start(f32[64,1280]{1,0:T(8,128)S(1)} %pad_maximum_fusion.1), channel_id=1, source_target_pairs={{0,1},{1,0},{2,3},{3,2},{4,5},{5,4},{6,7},{7,6},{8,9},{9,8},{10,11... | collective-permute-start | bytes 983048 | tf_op jit(solution)/shard_map/ppermute | solution.py:17
  24.2 8.6 %collective-permute-done.6 = f32[64,1280]{1,0:T(8,128)S(1)} collective-permute-done((f32[64,1280]{1,0:T(8,128)S(1)}, f32[64,1280]{1,0:T(8,128)S(1)}, u32[]{:S(2)}, u32[]{:S(2)}) %collective-permute-start.6) | collective-permute-done | bytes 327712 | tf_op jit(solution)/shard_map/ppermute | solution.py:17
  32.8 1.6 %collective-permute-start.9 = (f32[64,256]{1,0:T(8,128)S(1)}, f32[64,256]{1,0:T(8,128)S(1)}, u32[]{:S(2)}, u32[]{:S(2)}) collective-permute-start(f32[64,256]{1,0:T(8,128)S(1)} %slice_add_fusion.2), channel_id=1, source_target_pairs={{0,2},{1,3},{2,0},{3,1},{4,6},{5,7},{6,4},{7,5},{8,10},{9,11},{10,... | collective-permute-start | bytes 196616 | tf_op jit(solution)/shard_map/ppermute | solution.py:17
  34.5 0.1 add.29.rest_0_
  34.6 14.4 %shard_map.110 = (f32[2,1024,384]{2,1,0:T(8,128)S(1)}, f32[192,768]{1,0:T(8,128)S(1)}, f32[192,768]{1,0:T(8,128)S(1)}) custom-call(f32[2,1024,512]{2,1,0:T(8,128)} %inverse_far.3, f32[2,1024,768]{2,1,0:T(8,128)} %source_far.3, f32[2,1024,128]{2,1,0:T(8,128)} %one_far.3, f32[2,1024,128]{2,1,0:T(8,128)} %two_far.3, f32[2,1024,128]{2,1,0:T(8,128)} %three_far.3, ...), custom_call_target="tpu_custom_call" | custom-call | flops 8455716864 | bytes 7340032 | tf_op jit(solution)/shard_map/pallas_call | solution.py:332
  49.0 0.6 collective-permute-start.15
  49.6 0.6 collective-permute-start.7
  50.2 7.1 %collective-permute-done.15 = f32[96,768]{1,0:T(8,128)S(1)} collective-permute-done((f32[96,768]{1,0:T(8,128)S(1)}, f32[96,768]{1,0:T(8,128)S(1)}, u32[]{:S(2)}, u32[]{:S(2)}) %collective-permute-start.15) | collective-permute-done | bytes 294944 | tf_op jit(solution)/shard_map/ppermute | solution.py:17
  57.4 0.1 add.31
  57.5 0.6 collective-permute-start.4
  58.1 1.6 %collective-permute-start.16 = (f32[48,768]{1,0:T(8,128)S(1)}, f32[48,768]{1,0:T(8,128)S(1)}, u32[]{:S(2)}, u32[]{:S(2)}) collective-permute-start(f32[48,768]{1,0:T(8,128)S(1)} %get-tuple-element.67), channel_id=1, source_target_pairs={{0,1},{1,0},{2,3},{3,2},{4,5},{5,4},{6,7},{7,6},{8,9},{9,8},{10,11... | collective-permute-start | bytes 442376 | tf_op jit(solution)/shard_map/ppermute | solution.py:17
  59.6 0.1 collective-permute-start.10
  59.7 0.5 shard_map.111
  60.3 3.0 %collective-permute-done.16.refs_1_ = f32[48,768]{1,0:T(8,128)S(1)} collective-permute-done((f32[48,768]{1,0:T(8,128)S(1)}, f32[48,768]{1,0:T(8,128)S(1)}, u32[]{:S(2)}, u32[]{:S(2)}) %collective-permute-start.16) | collective-permute-done | bytes 147488 | tf_op jit(solution)/shard_map/ppermute | solution.py:17
  63.3 1.1 shard_map.116
  64.4 0.4 collective-permute-start.17
  64.7 0.2 collective-permute-done.4
  65.0 1.6 %collective-permute-start.5 = (f32[48,768]{1,0:T(8,128)S(1)}, f32[48,768]{1,0:T(8,128)S(1)}, u32[]{:S(2)}, u32[]{:S(2)}) collective-permute-start(f32[48,768]{1,0:T(8,128)S(1)} %get-tuple-element.69), channel_id=1, source_target_pairs={{0,1},{1,0},{2,3},{3,2},{4,5},{5,4},{6,7},{7,6},{8,9},{9,8},{10,11... | collective-permute-start | bytes 442376 | tf_op jit(solution)/shard_map/ppermute | solution.py:17
  66.6 0.5 shard_map.113
  67.1 2.0 %collective-permute-done.17.refs_1_ = f32[48,512]{1,0:T(8,128)S(1)} collective-permute-done((f32[48,512]{1,0:T(8,128)S(1)}, f32[48,512]{1,0:T(8,128)S(1)}, u32[]{:S(2)}, u32[]{:S(2)}) %collective-permute-start.17) | collective-permute-done | bytes 98336 | tf_op jit(solution)/shard_map/ppermute | solution.py:17
  69.0 1.1 shard_map.117
  70.2 3.2 %collective-permute-start.18 = (f32[48,256]{1,0:T(8,128)S(1)}, f32[48,256]{1,0:T(8,128)S(1)}, u32[]{:S(2)}, u32[]{:S(2)}) collective-permute-start(f32[48,256]{1,0:T(8,128)S(1)} %get-tuple-element.60.refs_0_), channel_id=1, source_target_pairs={{0,4},{1,5},{2,6},{3,7},{4,0},{5,1},{6,2},{7,3},{8,12},{9,13},{10,... | collective-permute-start | bytes 147464 | tf_op jit(solution)/shard_map/ppermute | solution.py:17
  73.3 2.2 %collective-permute-done.18.refs_1_ = f32[48,256]{1,0:T(8,128)S(1)} collective-permute-done((f32[48,256]{1,0:T(8,128)S(1)}, f32[48,256]{1,0:T(8,128)S(1)}, u32[]{:S(2)}, u32[]{:S(2)}) %collective-permute-start.18) | collective-permute-done | bytes 49184 | tf_op jit(solution)/shard_map/ppermute | solution.py:17
  75.5 0.3 shard_map.118
  75.9 1.7 %collective-permute-start.19 = (f32[48,768]{1,0:T(8,128)S(1)}, f32[48,768]{1,0:T(8,128)S(1)}, u32[]{:S(2)}, u32[]{:S(2)}) collective-permute-start(f32[48,768]{1,0:T(8,128)S(1)} %get-tuple-element.64), channel_id=1, source_target_pairs={{0,1},{1,0},{2,3},{3,2},{4,5},{5,4},{6,7},{7,6},{8,9},{9,8},{10,11... | collective-permute-start | bytes 442376 | tf_op jit(solution)/shard_map/ppermute | solution.py:17
  77.6 1.1 shard_map.112
  78.7 0.1 collective-permute-start.8
  78.8 4.8 %collective-permute-done.8.refs_1_ = f32[48,512]{1,0:T(8,128)S(1)} collective-permute-done((f32[48,512]{1,0:T(8,128)S(1)}, f32[48,512]{1,0:T(8,128)S(1)}, u32[]{:S(2)}, u32[]{:S(2)}) %collective-permute-start.8) | collective-permute-done | bytes 98336 | tf_op jit(solution)/shard_map/ppermute | solution.py:17
  83.6 1.1 shard_map.114
  84.7 2.5 %collective-permute-start.11 = (f32[48,256]{1,0:T(8,128)S(1)}, f32[48,256]{1,0:T(8,128)S(1)}, u32[]{:S(2)}, u32[]{:S(2)}) collective-permute-start(f32[48,256]{1,0:T(8,128)S(1)} %get-tuple-element.51.refs_0_), channel_id=1, source_target_pairs={{0,4},{1,5},{2,6},{3,7},{4,0},{5,1},{6,2},{7,3},{8,12},{9,13},{10,... | collective-permute-start | bytes 147464 | tf_op jit(solution)/shard_map/ppermute | solution.py:17
  87.2 1.6 %collective-permute-start.20 = (f32[96,768]{1,0:T(8,128)S(1)}, f32[96,768]{1,0:T(8,128)S(1)}, u32[]{:S(2)}, u32[]{:S(2)}) collective-permute-start(f32[96,768]{1,0:T(8,128)S(1)} %pad_maximum_fusion.3), channel_id=1, source_target_pairs={{0,16},{8,24},{16,0},{24,8},{1,17},{9,25},{17,1},{25,9},{2,18},{10... | collective-permute-start | bytes 884744 | tf_op jit(solution)/shard_map/ppermute | solution.py:17
  88.8 1.3 %collective-permute-done.11.refs_1_ = f32[48,256]{1,0:T(8,128)S(1)} collective-permute-done((f32[48,256]{1,0:T(8,128)S(1)}, f32[48,256]{1,0:T(8,128)S(1)}, u32[]{:S(2)}, u32[]{:S(2)}) %collective-permute-start.11) | collective-permute-done | bytes 49184 | tf_op jit(solution)/shard_map/ppermute | solution.py:17
  90.1 0.3 shard_map.115
  90.4 0.4 collective-permute-start.12
  90.9 4.7 %collective-permute-done.12 = f32[48,768]{1,0:T(8,128)S(1)} collective-permute-done((f32[48,768]{1,0:T(8,128)S(1)}, f32[48,768]{1,0:T(8,128)S(1)}, u32[]{:S(2)}, u32[]{:S(2)}) %collective-permute-start.12) | collective-permute-done | bytes 147488 | tf_op jit(solution)/shard_map/ppermute | solution.py:17
  95.6 1.5 %collective-permute-start.13 = (f32[96,768]{1,0:T(8,128)S(1)}, f32[96,768]{1,0:T(8,128)S(1)}, u32[]{:S(2)}, u32[]{:S(2)}) collective-permute-start(f32[96,768]{1,0:T(8,128)S(1)} %pad_maximum_fusion.2), channel_id=1, source_target_pairs={{0,16},{8,24},{16,0},{24,8},{1,17},{9,25},{17,1},{25,9},{2,18},{10... | collective-permute-start | bytes 884744 | tf_op jit(solution)/shard_map/ppermute | solution.py:17
  97.2 0.1 collective-permute-start.21
  97.3 5.1 %collective-permute-done.13 = f32[96,768]{1,0:T(8,128)S(1)} collective-permute-done((f32[96,768]{1,0:T(8,128)S(1)}, f32[96,768]{1,0:T(8,128)S(1)}, u32[]{:S(2)}, u32[]{:S(2)}) %collective-permute-start.13) | collective-permute-done | bytes 294944 | tf_op jit(solution)/shard_map/ppermute | solution.py:17
  102.5 0.1 collective-permute-start.14
  102.6 6.3 %shard_map.119.rest_0_ = f32[2,1024,768]{2,1,0:T(8,128)} custom-call(f32[2,1024,384]{2,1,0:T(8,128)S(1)} %get-tuple-element.58.solved, f32[192,768]{1,0:T(8,128)S(1)} %constant_dynamic-update-slice_fusion.3.kept, f32[192,768]{1,0:T(8,128)S(1)} %collective-permute-done.21.got, f32[2,1024,128]{2,1,0:T(8,128)S(1)} %copy-done, f32[2,1024,128]{2,1,0:T(8,128)S(1)} %copy-done.1, ...), custom_call_target="tpu_custom_call" | custom-call | flops 3623878656 | bytes 6291456 | tf_op jit(solution)/shard_map/pallas_call | solution.py:393
  108.9 6.3 %shard_map.120 = f32[2,1024,768]{2,1,0:T(8,128)} custom-call(f32[2,1024,384]{2,1,0:T(8,128)S(1)} %get-tuple-element.39.solved, f32[192,768]{1,0:T(8,128)S(1)} %constant_dynamic-update-slice_fusion.kept, f32[192,768]{1,0:T(8,128)S(1)} %collective-permute-done.14.got, f32[2,1024,128]{2,1,0:T(8,128)S(1)} %copy-done, ...), custom_call_target="tpu_custom_call", output_to_operand_aliasing={{}: (6, {})} | custom-call | flops 3623878656 | bytes 6291456 | tf_op jit(solution)/shard_map/pallas_call | solution.py:393
  (46 shorter events, 0.5 us)
Async XLA Ops:
  3.7 1.6 %collective-permute-start = (f32[64,768]{1,0:T(8,128)S(1)}, f32[64,768]{1,0:T(8,128)S(1)}, u32[]{:S(2)}, u32[]{:S(2)}) collective-permute-start(f32[64,768]{1,0:T(8,128)S(1)} %get-tuple-element.36), channel_id=1, source_target_pairs={{0,8},{8,0},{16,24},{24,16},{1,9},{9,1},{17,25},{25,17},{2,10},{10... | collective-permute-start | bytes 589832 | tf_op jit(solution)/shard_map/ppermute | solution.py:17
  5.4 17.2 %collective-permute-start.2 = (f32[64,768]{1,0:T(8,128)S(1)}, f32[64,768]{1,0:T(8,128)S(1)}, u32[]{:S(2)}, u32[]{:S(2)}) collective-permute-start(f32[64,768]{1,0:T(8,128)S(1)} %add.28.rest_0_), channel_id=1, source_target_pairs={{0,16},{8,24},{16,0},{24,8},{1,17},{9,25},{17,1},{25,9},{2,18},{10... | collective-permute-start | bytes 589832 | tf_op jit(solution)/shard_map/ppermute | solution.py:17
  22.5 12.0 %collective-permute-start.1 = (f32[192,768]{1,0:T(8,128)S(1)}, f32[192,768]{1,0:T(8,128)S(1)}, u32[]{:S(2)}, u32[]{:S(2)}) collective-permute-start(f32[192,768]{1,0:T(8,128)S(1)} %get-tuple-element.38), channel_id=1, source_target_pairs={{0,8},{8,0},{16,24},{24,16},{1,9},{9,1},{17,25},{25,17},{2,10},{10... | collective-permute-start | bytes 1769480 | tf_op jit(solution)/shard_map/ppermute | solution.py:17
  22.6 10.2 %collective-permute-start.6 = (f32[64,1280]{1,0:T(8,128)S(1)}, f32[64,1280]{1,0:T(8,128)S(1)}, u32[]{:S(2)}, u32[]{:S(2)}) collective-permute-start(f32[64,1280]{1,0:T(8,128)S(1)} %pad_maximum_fusion.1), channel_id=1, source_target_pairs={{0,1},{1,0},{2,3},{3,2},{4,5},{5,4},{6,7},{7,6},{8,9},{9,8},{10,11... | collective-permute-start | bytes 983048 | tf_op jit(solution)/shard_map/ppermute | solution.py:17
  32.8 26.8 %collective-permute-start.9 = (f32[64,256]{1,0:T(8,128)S(1)}, f32[64,256]{1,0:T(8,128)S(1)}, u32[]{:S(2)}, u32[]{:S(2)}) collective-permute-start(f32[64,256]{1,0:T(8,128)S(1)} %slice_add_fusion.2), channel_id=1, source_target_pairs={{0,2},{1,3},{2,0},{3,1},{4,6},{5,7},{6,4},{7,5},{8,10},{9,11},{10,... | collective-permute-start | bytes 196616 | tf_op jit(solution)/shard_map/ppermute | solution.py:17
  34.6 25.2 %copy-start.4 = (f32[2,128,256]{2,1,0:T(8,128)S(1)}, f32[2,128,256]{2,1,0:T(8,128)}, u32[]{:S(2)}) copy-start(f32[2,128,256]{2,1,0:T(8,128)} %core_one.1) | copy-start | bytes 786436
  49.0 17.6 %copy-start.3 = (f32[2,512,256]{2,1,0:T(8,128)S(1)}, f32[2,512,256]{2,1,0:T(8,128)}, u32[]{:S(2)}) copy-start(f32[2,512,256]{2,1,0:T(8,128)} %core_two.1) | copy-start | bytes 3145732
  49.0 17.6 %copy-start.5 = (f32[2,256,256]{2,1,0:T(8,128)S(1)}, f32[2,256,256]{2,1,0:T(8,128)}, u32[]{:S(2)}) copy-start(f32[2,256,256]{2,1,0:T(8,128)} %core_three.1) | copy-start | bytes 1572868
  49.0 8.3 %collective-permute-start.15 = (f32[96,768]{1,0:T(8,128)S(1)}, f32[96,768]{1,0:T(8,128)S(1)}, u32[]{:S(2)}, u32[]{:S(2)}) collective-permute-start(f32[96,768]{1,0:T(8,128)S(1)} %slice.70), channel_id=1, source_target_pairs={{0,16},{8,24},{16,0},{24,8},{1,17},{9,25},{17,1},{25,9},{2,18},{10... | collective-permute-start | bytes 884744 | tf_op jit(solution)/shard_map/ppermute | solution.py:17
  49.6 7.8 %collective-permute-start.3 = (f32[192,768]{1,0:T(8,128)S(1)}, f32[192,768]{1,0:T(8,128)S(1)}, u32[]{:S(2)}, u32[]{:S(2)}) collective-permute-start(f32[192,768]{1,0:T(8,128)S(1)} %get-tuple-element.41), channel_id=1, source_target_pairs={{0,8},{8,0},{16,24},{24,16},{1,9},{9,1},{17,25},{25,17},{2,10},{10... | collective-permute-start | bytes 1769480 | tf_op jit(solution)/shard_map/ppermute | solution.py:17
  49.6 10.1 %collective-permute-start.7 = (f32[64,1536]{1,0:T(8,128)S(1)}, f32[64,1536]{1,0:T(8,128)S(1)}, u32[]{:S(2)}, u32[]{:S(2)}) collective-permute-start(f32[64,1536]{1,0:T(8,128)S(1)} %pad_maximum_fusion.mine), channel_id=1, source_target_pairs={{0,8},{8,0},{16,24},{24,16},{1,9},{9,1},{17,25},{25,17},{2,10},{10... | collective-permute-start | bytes 1179656 | tf_op jit(solution)/shard_map/ppermute | solution.py:17
  57.5 7.5 %collective-permute-start.4 = (f32[96,768]{1,0:T(8,128)S(1)}, f32[96,768]{1,0:T(8,128)S(1)}, u32[]{:S(2)}, u32[]{:S(2)}) collective-permute-start(f32[96,768]{1,0:T(8,128)S(1)} %slice.61), channel_id=1, source_target_pairs={{0,16},{8,24},{16,0},{24,8},{1,17},{9,25},{17,1},{25,9},{2,18},{10... | collective-permute-start | bytes 884744 | tf_op jit(solution)/shard_map/ppermute | solution.py:17
  58.1 5.2 %collective-permute-start.16 = (f32[48,768]{1,0:T(8,128)S(1)}, f32[48,768]{1,0:T(8,128)S(1)}, u32[]{:S(2)}, u32[]{:S(2)}) collective-permute-start(f32[48,768]{1,0:T(8,128)S(1)} %get-tuple-element.67), channel_id=1, source_target_pairs={{0,1},{1,0},{2,3},{3,2},{4,5},{5,4},{6,7},{7,6},{8,9},{9,8},{10,11... | collective-permute-start | bytes 442376 | tf_op jit(solution)/shard_map/ppermute | solution.py:17
  59.6 7.0 %collective-permute-start.10 = (f32[64,512]{1,0:T(8,128)S(1)}, f32[64,512]{1,0:T(8,128)S(1)}, u32[]{:S(2)}, u32[]{:S(2)}) collective-permute-start(f32[64,512]{1,0:T(8,128)S(1)} %pad_maximum_fusion.4.mine), channel_id=1, source_target_pairs={{0,8},{8,0},{16,24},{24,16},{1,9},{9,1},{17,25},{25,17},{2,10},{10... | collective-permute-start | bytes 393224 | tf_op jit(solution)/shard_map/ppermute | solution.py:17
  64.4 4.7 %collective-permute-start.17 = (f32[48,512]{1,0:T(8,128)S(1)}, f32[48,512]{1,0:T(8,128)S(1)}, u32[]{:S(2)}, u32[]{:S(2)}) collective-permute-start(f32[48,512]{1,0:T(8,128)S(1)} %get-tuple-element.59.refs_0_), channel_id=1, source_target_pairs={{0,2},{1,3},{2,0},{3,1},{4,6},{5,7},{6,4},{7,5},{8,10},{9,11},{10,... | collective-permute-start | bytes 294920 | tf_op jit(solution)/shard_map/ppermute | solution.py:17
  65.0 37.5 %copy-start = (f32[2,1024,128]{2,1,0:T(8,128)S(1)}, f32[2,1024,128]{2,1,0:T(8,128)}, u32[]{:S(2)}) copy-start(f32[2,1024,128]{2,1,0:T(8,128)} %e_one.5) | copy-start | bytes 3145732
  65.0 37.5 %copy-start.1 = (f32[2,1024,128]{2,1,0:T(8,128)S(1)}, f32[2,1024,128]{2,1,0:T(8,128)}, u32[]{:S(2)}) copy-start(f32[2,1024,128]{2,1,0:T(8,128)} %e_two.5) | copy-start | bytes 3145732
  65.0 37.5 %copy-start.2 = (f32[2,1024,128]{2,1,0:T(8,128)S(1)}, f32[2,1024,128]{2,1,0:T(8,128)}, u32[]{:S(2)}) copy-start(f32[2,1024,128]{2,1,0:T(8,128)} %e_three.3) | copy-start | bytes 3145732
  65.0 12.5 %collective-permute-start.5 = (f32[48,768]{1,0:T(8,128)S(1)}, f32[48,768]{1,0:T(8,128)S(1)}, u32[]{:S(2)}, u32[]{:S(2)}) collective-permute-start(f32[48,768]{1,0:T(8,128)S(1)} %get-tuple-element.69), channel_id=1, source_target_pairs={{0,1},{1,0},{2,3},{3,2},{4,5},{5,4},{6,7},{7,6},{8,9},{9,8},{10,11... | collective-permute-start | bytes 442376 | tf_op jit(solution)/shard_map/ppermute | solution.py:17
  70.2 5.3 %collective-permute-start.18 = (f32[48,256]{1,0:T(8,128)S(1)}, f32[48,256]{1,0:T(8,128)S(1)}, u32[]{:S(2)}, u32[]{:S(2)}) collective-permute-start(f32[48,256]{1,0:T(8,128)S(1)} %get-tuple-element.60.refs_0_), channel_id=1, source_target_pairs={{0,4},{1,5},{2,6},{3,7},{4,0},{5,1},{6,2},{7,3},{8,12},{9,13},{10,... | collective-permute-start | bytes 147464 | tf_op jit(solution)/shard_map/ppermute | solution.py:17
  75.9 11.3 %collective-permute-start.19 = (f32[48,768]{1,0:T(8,128)S(1)}, f32[48,768]{1,0:T(8,128)S(1)}, u32[]{:S(2)}, u32[]{:S(2)}) collective-permute-start(f32[48,768]{1,0:T(8,128)S(1)} %get-tuple-element.64), channel_id=1, source_target_pairs={{0,1},{1,0},{2,3},{3,2},{4,5},{5,4},{6,7},{7,6},{8,9},{9,8},{10,11... | collective-permute-start | bytes 442376 | tf_op jit(solution)/shard_map/ppermute | solution.py:17
  78.7 4.9 %collective-permute-start.8 = (f32[48,512]{1,0:T(8,128)S(1)}, f32[48,512]{1,0:T(8,128)S(1)}, u32[]{:S(2)}, u32[]{:S(2)}) collective-permute-start(f32[48,512]{1,0:T(8,128)S(1)} %get-tuple-element.46.refs_0_), channel_id=1, source_target_pairs={{0,2},{1,3},{2,0},{3,1},{4,6},{5,7},{6,4},{7,5},{8,10},{9,11},{10,... | collective-permute-start | bytes 294920 | tf_op jit(solution)/shard_map/ppermute | solution.py:17
  84.7 5.4 %collective-permute-start.11 = (f32[48,256]{1,0:T(8,128)S(1)}, f32[48,256]{1,0:T(8,128)S(1)}, u32[]{:S(2)}, u32[]{:S(2)}) collective-permute-start(f32[48,256]{1,0:T(8,128)S(1)} %get-tuple-element.51.refs_0_), channel_id=1, source_target_pairs={{0,4},{1,5},{2,6},{3,7},{4,0},{5,1},{6,2},{7,3},{8,12},{9,13},{10,... | collective-permute-start | bytes 147464 | tf_op jit(solution)/shard_map/ppermute | solution.py:17
  87.2 10.0 %collective-permute-start.20 = (f32[96,768]{1,0:T(8,128)S(1)}, f32[96,768]{1,0:T(8,128)S(1)}, u32[]{:S(2)}, u32[]{:S(2)}) collective-permute-start(f32[96,768]{1,0:T(8,128)S(1)} %pad_maximum_fusion.3), channel_id=1, source_target_pairs={{0,16},{8,24},{16,0},{24,8},{1,17},{9,25},{17,1},{25,9},{2,18},{10... | collective-permute-start | bytes 884744 | tf_op jit(solution)/shard_map/ppermute | solution.py:17
  90.4 5.2 %collective-permute-start.12 = (f32[48,768]{1,0:T(8,128)S(1)}, f32[48,768]{1,0:T(8,128)S(1)}, u32[]{:S(2)}, u32[]{:S(2)}) collective-permute-start(f32[48,768]{1,0:T(8,128)S(1)} %get-tuple-element.57), channel_id=1, source_target_pairs={{0,1},{1,0},{2,3},{3,2},{4,5},{5,4},{6,7},{7,6},{8,9},{9,8},{10,11... | collective-permute-start | bytes 442376 | tf_op jit(solution)/shard_map/ppermute | solution.py:17
  95.6 6.8 %collective-permute-start.13 = (f32[96,768]{1,0:T(8,128)S(1)}, f32[96,768]{1,0:T(8,128)S(1)}, u32[]{:S(2)}, u32[]{:S(2)}) collective-permute-start(f32[96,768]{1,0:T(8,128)S(1)} %pad_maximum_fusion.2), channel_id=1, source_target_pairs={{0,16},{8,24},{16,0},{24,8},{1,17},{9,25},{17,1},{25,9},{2,18},{10... | collective-permute-start | bytes 884744 | tf_op jit(solution)/shard_map/ppermute | solution.py:17
  97.2 5.3 %collective-permute-start.21 = (f32[192,768]{1,0:T(8,128)S(1)}, f32[192,768]{1,0:T(8,128)S(1)}, u32[]{:S(2)}, u32[]{:S(2)}) collective-permute-start(f32[192,768]{1,0:T(8,128)S(1)} %constant_dynamic-update-slice_fusion.3.kept), channel_id=1, source_target_pairs={{0,8},{8,0},{16,24},{24,16},{1,9},{9,1},{17,25},{25,17},{2,10},{10... | collective-permute-start | bytes 1769480 | tf_op jit(solution)/shard_map/ppermute | solution.py:17
  102.5 6.4 %collective-permute-start.14 = (f32[192,768]{1,0:T(8,128)S(1)}, f32[192,768]{1,0:T(8,128)S(1)}, u32[]{:S(2)}, u32[]{:S(2)}) collective-permute-start(f32[192,768]{1,0:T(8,128)S(1)} %constant_dynamic-update-slice_fusion.kept), channel_id=1, source_target_pairs={{0,8},{8,0},{16,24},{24,16},{1,9},{9,1},{17,25},{25,17},{2,10},{10... | collective-permute-start | bytes 1769480 | tf_op jit(solution)/shard_map/ppermute | solution.py:17
